TPU v7x, 32 devices: a whole 2x2x4 slice. The times are simulated.
32 devices in a mesh: seq: 8 (over y, x, core), head: 4 (over z).
Axes of the slice: x: 2, y: 2, z: 4, core: 2. Of those that a mesh axis runs over, the one named last changes fastest.
Arguments:
- latent: bfloat16 [8, 1024, 2048], P('seq', None, 'head'), may hold values from -6 to 6
- modulation: float32 [9, 2048], replicated, may hold values from -3 to 3
- spatial_qkv: bfloat16 [3, 2048, 2048], P(None, None, 'head')
- spatial_out: bfloat16 [2048, 2048], P('head'), may hold values from -0.125 to 0.125
- temporal_qkv: bfloat16 [3, 2048, 2048], P(None, None, 'head')
- temporal_out: bfloat16 [2048, 2048], P('head'), may hold values from -0.125 to 0.125
- hidden_weight: bfloat16 [2048, 8192], P(None, 'head'), may hold values from -0.125 to 0.125
- output_weight: bfloat16 [8192, 2048], P('head'), may hold values from -0.0625 to 0.0625
Outputs:
- block_out: bfloat16 [8, 1024, 2048], P(None, 'seq', 'head')
All inputs are finite; a program needn't handle non-finite values.
Results may differ from a plain program's by a relative error of at most 0.009.
Values may be sent and summed in bfloat16 or wider, within the bound.
No kernel may reach another device: no remote copies, remote signals or barrier semaphores. Data moves between devices by JAX's collectives and lax.ppermute only.
A program may use at most 128 MiB of HBM per device.

v0:
```python
import jax
import jax.numpy as jnp
from jax import lax
from jax.sharding import PartitionSpec as P

HD = 64


def layer_norm(values):
    average = jnp.mean(values, axis=-1, keepdims=True)
    centred = values - average
    variance = jnp.mean(centred * centred, axis=-1, keepdims=True)
    return centred * lax.rsqrt(variance + 1e-06)


def modulate(stream, modulation, offset):
    normed = layer_norm(stream.astype(jnp.float32))
    return (normed * (1.0 + modulation[offset + 1]) + modulation[offset]).astype(jnp.bfloat16)


def attend(query, keys, values):
    scores = jnp.einsum(
        "glhd,gmhd->ghlm", query, keys, preferred_element_type=jnp.float32
    ) * HD ** (-0.5)
    attn_weights = jax.nn.softmax(scores, axis=-1).astype(jnp.bfloat16)
    return jnp.einsum(
        "ghlm,gmhd->glhd", attn_weights, values, preferred_element_type=jnp.float32
    ).astype(jnp.bfloat16)


def project_three(normed, weights):
    return [
        jnp.dot(normed, weights[member], preferred_element_type=jnp.float32).astype(jnp.bfloat16)
        for member in range(3)
    ]


def column_adder(columns, portion):
    return jnp.dot(portion, columns, preferred_element_type=jnp.float32)


def per_device(
    latent,
    modulation,
    spatial_qkv,
    spatial_out,
    temporal_qkv,
    temporal_out,
    hidden_weight,
    output_weight,
):
    width_local = latent.shape[2]
    heads_local = width_local // HD
    anchor = lax.axis_index("head") * width_local
    local_rows = lax.dynamic_slice_in_dim(modulation, anchor, width_local, 1)
    full_spatial = lax.all_gather(latent, "head", axis=2, tiled=True)
    normed = modulate(full_spatial, modulation, 0)
    frames_local = latent.shape[0]
    patches = latent.shape[1]
    query, keys, values = [
        member.reshape(frames_local, patches, heads_local, HD)
        for member in project_three(normed, spatial_qkv)
    ]
    spatial = lax.map(
        lambda triple: attend(triple[0][None], triple[1][None], triple[2][None])[0],
        (query, keys, values),
    )
    spatial = spatial.reshape(frames_local, patches, width_local)
    columns = lax.all_to_all(spatial_out, "head", split_axis=1, concat_axis=0, tiled=True)
    reduced = column_adder(columns, lax.all_gather(spatial, "head", axis=2, tiled=True))
    stream_one = (latent.astype(jnp.float32) + local_rows[2] * reduced).astype(jnp.bfloat16)
    full_stream = lax.all_gather(stream_one, "head", axis=2, tiled=True)
    normed = modulate(full_stream, modulation, 3)
    stacked = jnp.stack(project_three(normed, temporal_qkv), axis=2)
    moved, stream_temporal = (
        lax.all_to_all(stacked, "seq", split_axis=1, concat_axis=0, tiled=True),
        lax.all_to_all(stream_one, "seq", split_axis=1, concat_axis=0, tiled=True),
    )
    query, keys, values = (moved[:, :, 0], moved[:, :, 1], moved[:, :, 2])
    frames = stream_temporal.shape[0]
    patches_local = stream_temporal.shape[1]

    def to_groups(tensor):
        return jnp.transpose(tensor.reshape(frames, patches_local, heads_local, HD), (1, 0, 2, 3))

    temporal = attend(to_groups(query), to_groups(keys), to_groups(values))
    temporal = jnp.transpose(temporal, (1, 0, 2, 3)).reshape(frames, patches_local, width_local)
    columns = lax.all_to_all(temporal_out, "head", split_axis=1, concat_axis=0, tiled=True)
    reduced = column_adder(columns, lax.all_gather(temporal, "head", axis=2, tiled=True))
    stream_two = (stream_temporal.astype(jnp.float32) + local_rows[5] * reduced).astype(
        jnp.bfloat16
    )
    full_two = lax.all_gather(stream_two, "head", axis=2, tiled=True)
    normed = modulate(full_two, modulation, 6)
    pre_act = jnp.dot(normed, hidden_weight, preferred_element_type=jnp.float32)
    hidden = jax.nn.gelu(pre_act, approximate=True).astype(jnp.bfloat16)
    partial_sums = jnp.dot(hidden, output_weight, preferred_element_type=jnp.float32)
    reduced = lax.psum_scatter(partial_sums, "head", scatter_dimension=2, tiled=True)
    return (stream_two.astype(jnp.float32) + local_rows[8] * reduced).astype(jnp.bfloat16)


def solution(mesh):
    in_specs = (
        P("seq", None, "head"),
        P(),
        P(None, None, "head"),
        P("head", None),
        P(None, None, "head"),
        P("head", None),
        P(None, "head"),
        P("head", None),
    )
    out_specs = P(None, "seq", "head")
    return jax.shard_map(
        per_device, mesh=mesh, in_specs=in_specs, out_specs=out_specs, check_vma=False
    )
```

profile of v0, /device:TPU:0, one launch (start us, length us, event | category | flops | bytes accessed | tf_op | source)
XLA Modules:
  0.0 838.2 jit_solution(230585978647317202)
XLA Ops:
  7.3 1.7 slice_add_fusion
  9.0 83.4 %all-gather.6.cloned.1.call-done = bf16[1,1024,2048]{2,1,0:T(8,128)(2,1)} async-done(((bf16[1,1024,512]{2,1,0:T(8,128)(2,1)}), bf16[1,1024,2048]{2,1,0:T(8,128)(2,1)}) %all-gather.6.cloned.1.call-update) | async-done | bytes 4194320 | tf_op jit(solution)/shard_map/all_gather | solution.py:56
  92.4 3.0 convert_reduce_fusion.2
  97.1 1.9 fusion.42
  99.0 2.4 fusion.95
  101.4 2.4 fusion.98
  103.8 2.4 fusion.101
  106.3 14.6 %fusion.131 = (f32[8,1024]{1,0:T(8,128)S(1)}, f32[8,1024,1024]{1,2,0:T(8,128)}) fusion(bf16[1024,8,64]{0,2,1:T(8,128)(2,1)S(1)} %bitcast.158, bf16[1024,8,64]{0,2,1:T(8,128)(2,1)S(1)} %bitcast.159), kind=kOutput, calls=%fused_computation.121 | convolution fusion | flops 1098908672 | bytes 35684352 | tf_op jit(solution)/shard_map/while/body/eval_jaxpr/sub | solution.py:25
  120.9 13.4 %fusion.113 = bf16[8,64,1024]{2,1,0:T(8,128)(2,1)} fusion(bf16[1024,8,64]{0,2,1:T(8,128)(2,1)S(1)} %bitcast.157, f32[8,1024,1024]{1,2,0:T(8,128)} %get-tuple-element.33, f32[8,1024]{1,0:T(8,128)S(1)} %get-tuple-element.32), kind=kOutput, calls=%fused_computation.100 | convolution fusion | flops 1091043328 | bytes 35684352 | tf_op jit(solution)/shard_map/while/body/eval_jaxpr/ghlm,gmhd->glhd/dot_general | solution.py:26
  134.3 2.5 copy.49
  136.8 3.8 all-to-all-start
  141.7 100.5 %all-to-all-done = bf16[512,4,512]{0,2,1:T(8,128)(2,1)S(1)} async-done(((bf16[512,4,512]{0,2,1:T(8,128)(2,1)}), bf16[512,4,512]{0,2,1:T(8,128)(2,1)S(1)}, u32[]{:S(2)}, u32[]{:S(2)}) %all-to-all-start) | async-done | bytes 2097184 | tf_op jit(solution)/shard_map/all_to_all | solution.py:69
  242.2 2.4 copy.50
  244.6 12.0 %all-gather.8.cloned.1.call-done = bf16[1,1024,2048]{1,2,0:T(8,128)(2,1)} async-done(((bf16[1,1024,512]{1,2,0:T(8,128)(2,1)}), bf16[1,1024,2048]{1,2,0:T(8,128)(2,1)}) %all-gather.8.cloned.1.call-update) | async-done | bytes 4194320 | tf_op jit(solution)/shard_map/all_gather | solution.py:70
  256.6 6.2 fusion.76
  262.9 79.9 %all-gather.10.cloned.1.call-done = bf16[1,1024,2048]{2,1,0:T(8,128)(2,1)} async-done(((bf16[1,1024,512]{2,1,0:T(8,128)(2,1)}), bf16[1,1024,2048]{2,1,0:T(8,128)(2,1)}) %all-gather.10.cloned.1.call-update) | async-done | bytes 4194320 | tf_op jit(solution)/shard_map/all_gather | solution.py:72
  342.8 3.0 convert_reduce_fusion.1
  347.5 1.9 fusion.43
  349.8 2.3 fusion.114
  352.1 2.3 fusion.117
  354.4 2.3 fusion.120
  357.1 2.7 copy.52
  359.8 52.9 %all_to_all.59 = bf16[1,1024,3,512]{3,2,0,1:T(4,128)(2,1)S(1)} all-to-all(bf16[1,1024,3,512]{3,2,0,1:T(4,128)(2,1)S(1)} %copy.52), channel_id=1, replica_groups=mesh['seq'=8,'head'=4] {'seq'}, dimensions={1} | all-to-all | bytes 6291456 | tf_op jit(solution)/shard_map/all_to_all | solution.py:76
  413.5 1.5 fusion.129
  415.7 3.0 copy.59
  418.7 1.6 copy.56
  420.3 3.8 copy.57
  424.1 2.8 fusion.66
  426.9 4.6 fusion.132
  432.2 3.0 copy.55
  435.2 4.2 convert_bitcast_fusion
  439.4 3.3 copy.61
  442.7 1.5 copy.62
  444.3 1.6 copy.71
  446.4 7.0 reduce.8
  453.5 1.6 reshape.197
  455.1 3.6 all-to-all-start.1
  458.6 1.6 copy.70
  460.2 13.7 %all-to-all-done.1 = bf16[8,2,32768]{2,1,0:T(2,128)(2,1)S(1)} async-done(((bf16[8,2,32768]{2,1,0:T(2,128)(2,1)}), bf16[8,2,32768]{2,1,0:T(2,128)(2,1)S(1)}, u32[]{:S(2)}, u32[]{:S(2)}) %all-to-all-start.1) | async-done | bytes 1048608 | tf_op jit(solution)/shard_map/all_to_all | solution.py:77
  473.9 4.4 all-to-all-start.3
  479.5 1.6 copy.66
  481.1 85.2 %all-to-all-done.3 = bf16[512,4,512]{2,0,1:T(8,128)(2,1)} async-done(((bf16[512,4,512]{2,0,1:T(8,128)(2,1)}), bf16[512,4,512]{2,0,1:T(8,128)(2,1)}, u32[]{:S(2)}, u32[]{:S(2)}) %all-to-all-start.3) | async-done | bytes 2097184 | tf_op jit(solution)/shard_map/all_to_all | solution.py:88
  566.2 6.7 add_convert_fusion.1
  573.3 79.0 %all-gather.14.cloned.1.call-done = bf16[8,128,2048]{2,1,0:T(8,128)(2,1)} async-done(((bf16[8,128,512]{2,1,0:T(8,128)(2,1)}), bf16[8,128,2048]{2,1,0:T(8,128)(2,1)}) %all-gather.14.cloned.1.call-update) | async-done | bytes 4194320 | tf_op jit(solution)/shard_map/all_gather | solution.py:93
  652.3 3.0 convert_reduce_fusion
  657.0 27.8 %fusion.33 = f32[8,128,2048]{2,1,0:T(8,128)} fusion(bf16[2048,2048]{1,0:T(8,128)(2,1)} %param.15, bf16[2048,2048]{1,0:T(8,128)(2,1)} %param.14, bf16[8,128,2048]{2,1,0:T(8,128)(2,1)} %all-gather.14.cloned.1.call-done, f32[2048]{0:T(1024)S(1)} %bitcast.150, f32[2048]{0:T(1024)S(1)} %bitcast.149, f32[8,128]{1,0:T(8,128)S(1)} %add_rsqrt_fusion, ...), kind=kOutput, calls=%fused_computation.41 | convolution fusion | flops 17211326464 | bytes 29384704 | tf_op jit(solution)/shard_map/dot_general | solution.py:97
  684.8 143.3 %reduce-scatter.2.cloned.1.call-done = f32[8,128,512]{2,1,0:T(8,128)} async-done(((f32[8,128,2048]{2,1,0:T(8,128)}), f32[8,128,512]{2,1,0:T(8,128)}) %reduce-scatter.2.cloned.1.call-update) | async-done | bytes 2097168 | tf_op jit(solution)/shard_map/reduce_scatter | solution.py:98
  828.1 2.9 add_convert_fusion
  (61 shorter events, 11.9 us)
Async XLA Ops:
  6.5 85.9 %all-gather.6.cloned.1.call-start = ((), (), s32[]{:S(2)}) async-start(), calls=%async_computation.5 | async-start | bytes 5242880 | tf_op jit(solution)/shard_map/all_gather | solution.py:56
  7.3 249.4 %all-gather.8.cloned.1.call-start = ((), (), s32[]{:S(2)}) async-start(), calls=%async_computation.6 | async-start | bytes 5242880 | tf_op jit(solution)/shard_map/all_gather | solution.py:70
  92.4 3.4 copy-start
  95.8 3.1 slice-start
  97.1 1.9 slice-start.1
  120.9 13.4 %copy-start.6 = (bf16[512,2048]{1,0:T(8,128)(2,1)S(1)}, bf16[512,2048]{1,0:T(8,128)(2,1)}, u32[]{:S(2)}) copy-start(bf16[512,2048]{1,0:T(8,128)(2,1)} %param.11) | copy-start | bytes 6291460
  136.8 119.8 %copy-start.8 = (bf16[1,1024,512]{2,1,0:T(8,128)(2,1)S(1)}, bf16[1,1024,512]{2,1,0:T(8,128)(2,1)}, u32[]{:S(2)}) copy-start(bf16[1,1024,512]{2,1,0:T(8,128)(2,1)} %param.8) | copy-start | bytes 3145732
  136.8 105.4 %all-to-all-start = ((bf16[512,4,512]{0,2,1:T(8,128)(2,1)}), bf16[512,4,512]{0,2,1:T(8,128)(2,1)S(1)}, u32[]{:S(2)}, u32[]{:S(2)}) async-start(bf16[512,4,512]{0,2,1:T(8,128)(2,1)} %bitcast.133), calls=%async_computation | async-start | bytes 4194304 | tf_op jit(solution)/shard_map/all_to_all | solution.py:69
  140.6 202.2 %all-gather.10.cloned.1.call-start = ((), (), s32[]{:S(2)}) async-start(), calls=%async_computation.7 | async-start | bytes 5242880 | tf_op jit(solution)/shard_map/all_gather | solution.py:72
  262.8 303.4 %all-gather.12.cloned.1.call-start = ((), (), s32[]{:S(2)}) async-start(), calls=%async_computation.8 | async-start | bytes 5242880 | tf_op jit(solution)/shard_map/all_gather | solution.py:89
  342.8 3.4 copy-start.1
  346.3 3.1 slice-start.2
  347.5 2.3 slice-start.3
  426.9 4.7 copy-start.5
  439.4 4.8 copy-start.3
  453.5 5.2 copy-start.7
  455.1 18.9 %all-to-all-start.1 = ((bf16[8,2,32768]{2,1,0:T(2,128)(2,1)}), bf16[8,2,32768]{2,1,0:T(2,128)(2,1)S(1)}, u32[]{:S(2)}, u32[]{:S(2)}) async-start(bf16[8,2,32768]{2,1,0:T(2,128)(2,1)} %reshape.197), calls=%async_computation.1 | async-start | bytes 2097152 | tf_op jit(solution)/shard_map/all_to_all | solution.py:77
  473.9 92.3 %all-to-all-start.3 = ((bf16[512,4,512]{2,0,1:T(8,128)(2,1)}), bf16[512,4,512]{2,0,1:T(8,128)(2,1)}, u32[]{:S(2)}, u32[]{:S(2)}) async-start(bf16[512,4,512]{2,0,1:T(8,128)(2,1)} %bitcast.129), calls=%async_computation.3 | async-start | bytes 4194304 | tf_op jit(solution)/shard_map/all_to_all | solution.py:88
  478.4 173.9 %all-gather.14.cloned.1.call-start = ((), (), s32[]{:S(2)}) async-start(), calls=%async_computation.9 | async-start | bytes 5242880 | tf_op jit(solution)/shard_map/all_gather | solution.py:93
  573.0 84.0 %copy-start.10 = (f32[1,2048]{1,0:T(1,128)S(1)}, f32[1,2048]{1,0:T(1,128)}, u32[]{:S(2)}) copy-start(f32[1,2048]{1,0:T(1,128)} %get-tuple-element.31) | copy-start | bytes 24580
  573.0 84.0 %copy-start.9 = (f32[1,2048]{1,0:T(1,128)S(1)}, f32[1,2048]{1,0:T(1,128)}, u32[]{:S(2)}) copy-start(f32[1,2048]{1,0:T(1,128)} %get-tuple-element.26) | copy-start | bytes 24580
  573.0 255.1 %reduce-scatter.2.cloned.1.call-start = ((), (), s32[]{:S(2)}) async-start(), calls=%async_computation.10 | async-start | bytes 10485760 | tf_op jit(solution)/shard_map/reduce_scatter | solution.py:98
  652.3 3.4 copy-start.2
  684.8 143.3 %copy-start.4 = (bf16[8,128,512]{2,1,0:T(8,128)(2,1)S(1)}, bf16[8,128,512]{2,1,0:T(8,128)(2,1)}, u32[]{:S(2)}) copy-start(bf16[8,128,512]{2,1,0:T(8,128)(2,1)} %add_convert_fusion.1) | copy-start | bytes 3145732
Sparse Core Ops, SparseCore 0:
  8.9 83.4 all-gather.5
  134.4 122.1 all-gather.7
  263.0 79.7 all-gather.9
  444.4 121.0 all-gather.11
  573.1 79.1 all-gather.13
  685.0 143.0 reduce-scatter.1
where the time goes:
time: 849 us; the launch traced here: 838 us
  waiting for transfers between devices  598 us (70%)
  matrix products  90 us (11%)
  blocking collectives  52.9 us (6%)
  local copies, waits for them, and re-layouts  38 us (4%)
  other arithmetic  33 us (4%)
  between operations  14.2 us (2%)
  starting transfers between devices  12.4 us (1%)
    reduce_scatter x1, waiting for transfers between devices, per_device(): lax.psum_scatter(partial_sums, 'head', scatter_dimension=2, tiled=True)  143 us
    all_to_all x1, waiting for transfers between devices, per_device(): lax.all_to_all(spatial_out, 'head', split_axis=1, concat_axis=0, tiled=True)  100 us
    all_to_all x1, waiting for transfers between devices, per_device(): lax.all_to_all(temporal_out, 'head', split_axis=1, concat_axis=0, tiled=T...  85.2 us
    all_gather x1, waiting for transfers between devices, per_device(): full_spatial = lax.all_gather(latent, 'head', axis=2, tiled=True)  83.4 us
    all_gather x1, waiting for transfers between devices, per_device(): full_stream = lax.all_gather(stream_one, 'head', axis=2, tiled=True)  79.9 us
    all_gather x1, waiting for transfers between devices, per_device(): full_two = lax.all_gather(stream_two, 'head', axis=2, tiled=True)  79 us
    all_to_all x1, blocking collectives, per_device(): lax.all_to_all(stacked, 'seq', split_axis=1, concat_axis=0, tiled=True)  52.9 us
    dot_general x1, matrix products, per_device(): jnp.dot(hidden, output_weight, preferred_element_type=jnp.float32)  27.8 us
  transfers between devices with their start and end apart: 9, of which 8 were waited for; matrix products, arithmetic and copies ran while one was open for 3% of the time, Pallas kernels for 0%

commit v1 on v0

v1 whole, which is shorter than its diff:
```python
import functools

import jax
import jax.numpy as jnp
from jax import lax
from jax.experimental import pallas as pl
from jax.experimental.pallas import tpu as pltpu
from jax.sharding import PartitionSpec as P

HD = 64
LANES = 128


def modulate(stream, modulation, offset):
    values = stream.astype(jnp.float32)
    average = jnp.mean(values, axis=-1, keepdims=True)
    centred = values - average
    variance = jnp.mean(centred * centred, axis=-1, keepdims=True)
    normed = centred * lax.rsqrt(variance + 1e-06)
    return (normed * (1.0 + modulation[offset + 1]) + modulation[offset]).astype(jnp.bfloat16)


def spatial_kernel(query_ref, key_ref, value_ref, out_ref):
    pieces = []
    for head in range(query_ref.shape[1] // HD):
        span = slice(head * HD, (head + 1) * HD)
        query = query_ref[:, span] * jnp.bfloat16(HD ** (-0.5))
        scores = lax.dot_general(
            query, key_ref[:, span], (((1,), (1,)), ((), ())), preferred_element_type=jnp.float32
        )
        top = jnp.max(scores, axis=-1, keepdims=True)
        raised = jnp.exp(scores - top)
        total = jnp.sum(raised, axis=-1, keepdims=True)
        mixed = jnp.dot(
            raised.astype(jnp.bfloat16), value_ref[:, span], preferred_element_type=jnp.float32
        )
        pieces.append((mixed / total).astype(jnp.bfloat16))
    out_ref[...] = jnp.concatenate(pieces, axis=-1)


def spatial_attention(query, keys, values):
    tokens, width = query.shape
    rows = min(tokens, 512)
    return pl.pallas_call(
        spatial_kernel,
        grid=(width // LANES, tokens // rows),
        in_specs=[
            pl.BlockSpec((rows, LANES), lambda i, j: (j, i)),
            pl.BlockSpec((tokens, LANES), lambda i, j: (0, i)),
            pl.BlockSpec((tokens, LANES), lambda i, j: (0, i)),
        ],
        out_specs=pl.BlockSpec((rows, LANES), lambda i, j: (j, i)),
        out_shape=jax.ShapeDtypeStruct((tokens, width), jnp.bfloat16),
        name="spatial_attention",
    )(query, keys, values)


def temporal_kernel(query_ref, key_ref, value_ref, out_ref):
    _, frames, rows, width = query_ref.shape
    feature = lax.broadcasted_iota(jnp.int32, (width, LANES), 0) // HD
    member = lax.broadcasted_iota(jnp.int32, (width, LANES), 1)
    gather = jnp.where(feature == member, 1.0, 0.0).astype(jnp.bfloat16)
    feature = lax.broadcasted_iota(jnp.int32, (LANES, width), 1) // HD
    member = lax.broadcasted_iota(jnp.int32, (LANES, width), 0)
    spread = jnp.where(feature == member, 1.0, 0.0).astype(jnp.bfloat16)
    for frame in range(frames):
        query = query_ref[0, frame]
        products = jnp.concatenate([query * key_ref[0, other] for other in range(frames)], axis=0)
        scores = jnp.dot(products, gather, preferred_element_type=jnp.float32) * HD ** (-0.5)
        scores = [scores[other * rows : (other + 1) * rows] for other in range(frames)]
        top = functools.reduce(jnp.maximum, scores)
        raised = [jnp.exp(score - top) for score in scores]
        total = functools.reduce(jnp.add, raised)
        shares = jnp.concatenate([(part / total).astype(jnp.bfloat16) for part in raised], axis=0)
        spread_out = jnp.dot(shares, spread, preferred_element_type=jnp.float32)
        mixed = functools.reduce(
            jnp.add,
            [
                spread_out[other * rows : (other + 1) * rows]
                * value_ref[0, other].astype(jnp.float32)
                for other in range(frames)
            ],
        )
        out_ref[0, frame] = mixed.astype(jnp.bfloat16)


def temporal_attention(query, keys, values):
    groups, frames, rows, width = query.shape
    block = pl.BlockSpec((1, frames, rows, width), lambda i: (i, 0, 0, 0))
    return pl.pallas_call(
        temporal_kernel,
        grid=(groups,),
        in_specs=[block] * 3,
        out_specs=block,
        out_shape=jax.ShapeDtypeStruct(query.shape, jnp.bfloat16),
        name="temporal_attention",
    )(query, keys, values)


def project_three(normed, weights):
    return [
        jnp.dot(normed, weights[member], preferred_element_type=jnp.float32).astype(jnp.bfloat16)
        for member in range(3)
    ]


def whole_weight(shard, seq, head):
    rows, columns = shard.shape
    part = rows // seq
    mine = lax.dynamic_slice_in_dim(shard, lax.axis_index("seq") * part, part, 0)
    gathered = lax.all_gather(mine, ("seq", "head"), axis=0, tiled=True)
    gathered = gathered.reshape(seq, head, part, columns)
    return jnp.transpose(gathered, (1, 0, 2, 3)).reshape(head * rows, columns)


def to_tokens(features, head):
    tokens, width = features.shape
    pieces = features.reshape(head, tokens // head, width)
    pieces = lax.all_to_all(pieces, "head", split_axis=0, concat_axis=0, tiled=True)
    return jnp.transpose(pieces, (1, 0, 2)).reshape(tokens // head, head * width)


def per_device(
    seq,
    head,
    latent,
    modulation,
    spatial_qkv,
    spatial_out,
    temporal_qkv,
    temporal_out,
    hidden_weight,
    output_weight,
):
    patches = latent.shape[1]
    width_local = latent.shape[2]
    width = modulation.shape[1]
    own = lax.axis_index("head")
    rows = patches // (seq * head)
    frames = seq * latent.shape[0]
    share = patches // head

    ordered = jnp.transpose(latent[0].reshape(seq, head, rows, width_local), (1, 0, 2, 3))
    ordered = ordered.reshape(patches, width_local)
    full = lax.all_gather(ordered, "head", axis=1, tiled=True)
    spatial_whole = whole_weight(spatial_out, seq, head)
    query, keys, values = project_three(modulate(full, modulation, 0), spatial_qkv)
    spatial = to_tokens(spatial_attention(query, keys, values), head)
    branch = jnp.dot(spatial, spatial_whole, preferred_element_type=jnp.float32)
    mine = lax.dynamic_slice_in_dim(full, own * share, share, 0)
    stream_one = (mine.astype(jnp.float32) + modulation[2] * branch).astype(jnp.bfloat16)

    stream_one = lax.all_to_all(
        stream_one.reshape(seq, rows, width), "seq", split_axis=0, concat_axis=0, tiled=True
    ).reshape(frames * rows, width)
    temporal_in = lax.all_gather(modulate(stream_one, modulation, 3), "head", axis=0, tiled=True)
    temporal_whole = whole_weight(temporal_out, seq, head)
    query, keys, values = [
        member.reshape(head, frames, rows, width_local)
        for member in project_three(temporal_in, temporal_qkv)
    ]
    temporal = temporal_attention(query, keys, values)
    temporal = to_tokens(temporal.reshape(head * frames * rows, width_local), head)
    branch = jnp.dot(temporal, temporal_whole, preferred_element_type=jnp.float32)
    stream_two = (stream_one.astype(jnp.float32) + modulation[5] * branch).astype(jnp.bfloat16)

    hidden_in = lax.all_gather(modulate(stream_two, modulation, 6), "head", axis=0, tiled=True)
    residual = jnp.transpose(stream_two.reshape(frames * rows, head, width_local), (1, 0, 2))
    residual = lax.all_to_all(residual, "head", split_axis=0, concat_axis=0, tiled=True)
    pre_act = jnp.dot(hidden_in, hidden_weight, preferred_element_type=jnp.float32)
    hidden = jax.nn.gelu(pre_act, approximate=True).astype(jnp.bfloat16)
    partial_sums = jnp.dot(hidden, output_weight, preferred_element_type=jnp.float32)
    reduced = lax.psum_scatter(
        partial_sums.astype(jnp.bfloat16), "head", scatter_dimension=1, tiled=True
    )
    gate = lax.dynamic_slice_in_dim(modulation[8], own * width_local, width_local, 0)
    out = residual.reshape(head * frames * rows, width_local).astype(jnp.float32)
    out = (out + gate * reduced.astype(jnp.float32)).astype(jnp.bfloat16)
    out = jnp.transpose(out.reshape(head, frames, rows, width_local), (1, 0, 2, 3))
    return out.reshape(frames, head * rows, width_local)


def solution(mesh):
    in_specs = (
        P("seq", None, "head"),
        P(),
        P(None, None, "head"),
        P("head", None),
        P(None, None, "head"),
        P("head", None),
        P(None, "head"),
        P("head", None),
    )
    out_specs = P(None, "seq", "head")
    return jax.shard_map(
        functools.partial(per_device, mesh.shape["seq"], mesh.shape["head"]),
        mesh=mesh,
        in_specs=in_specs,
        out_specs=out_specs,
        check_vma=False,
    )
```

time: 849 us -> 615 us (0.72)
  waiting for transfers between devices: 598 us -> 431 us
  blocking collectives: 52.9 us -> 18.3 us
  Pallas kernels: 0 us -> 30.4 us
  matrix products: 90 us -> 63.4 us
  other arithmetic: 33 us -> 12.9 us
  local copies, waits for them, and re-layouts: 38 us -> 28.7 us
    all_to_all x3, waiting for transfers between devices: 199 us -> 54.3 us  [the longest x1 54.3 us: per_device(): lax.all_to_all(residual, 'head', split_axis=0, concat_axis=0, tiled=True)]
    reduce_scatter x1, waiting for transfers between devices: 143 us -> 33.4 us  [per_device(): lax.psum_scatter(partial_sums.astype(jnp.bfloat16), 'head', scatter_dimen...]
    all_gather x5, waiting for transfers between devices: 254 us -> 344 us  [the longest x2 107 us: whole_weight(): gathered = lax.all_gather(mine, ('seq', 'head'), axis=0, tiled=True)]
    all_to_all x1, blocking collectives: 52.9 us -> 18.3 us  [per_device(): lax.all_to_all(stream_one.reshape(seq, rows, width), 'seq', split_axis=0,...]
    pallas_call x0 -> x2, Pallas kernels: none -> 30.4 us  [the longest x1 18.6 us: spatial_attention(): pl.pallas_call(spatial_kernel, grid=(width // LANES, tokens // rows), in_...]
    dot_general x5 -> x2, matrix products: 33.4 us -> 11.8 us  [the longest x1 5.96 us: per_device(): branch = jnp.dot(spatial, spatial_whole, preferred_element_type=jnp.float32)]
    transpose x0 -> x3, local copies, waits for them, and re-layouts: none -> 17.6 us  [the longest x2 16.5 us: whole_weight(): return jnp.transpose(gathered, (1, 0, 2, 3)).reshape(head * rows, columns)]
    sub x1 -> x0, matrix products: 14.6 us -> none  [attend(): attn_weights = jax.nn.softmax(scores, axis=-1).astype(jnp.bfloat16)]
  transfers between devices with their start and end apart: 9 -> 9, of which waited for: 8 -> 7; matrix products, arithmetic and copies ran while one was open for 3% -> 10% of each run, Pallas kernels for 0% -> 5%
where the time goes in v1:
time: 615 us; the launch traced here: 610 us
  waiting for transfers between devices  431 us (70%)
  matrix products  63.4 us (10%)
  Pallas kernels  30.4 us (5%)
  local copies, waits for them, and re-layouts  28.7 us (5%)
  blocking collectives  18.3 us (3%)
  between operations  13.6 us (2%)
  other arithmetic  12.9 us (2%)
  starting transfers between devices  11.2 us (2%)
    all_gather x2, waiting for transfers between devices, whole_weight(): gathered = lax.all_gather(mine, ('seq', 'head'), axis=0, tiled=True)  107 us
    all_gather x1, waiting for transfers between devices, per_device(): full = lax.all_gather(ordered, 'head', axis=1, tiled=True)  81.5 us
    all_gather x1, waiting for transfers between devices, per_device(): lax.all_gather(modulate(stream_two, modulation, 6), 'head', axis=0, tiled...  79.1 us
    all_gather x1, waiting for transfers between devices, per_device(): lax.all_gather(modulate(stream_one, modulation, 3), 'head', axis=0, tiled...  76.2 us
    all_to_all x1, waiting for transfers between devices, per_device(): lax.all_to_all(residual, 'head', split_axis=0, concat_axis=0, tiled=True)  54.3 us
    reduce_scatter x1, waiting for transfers between devices, per_device(): lax.psum_scatter(partial_sums.astype(jnp.bfloat16), 'head', scatter_dimen...  33.4 us
    dot_general x6, matrix products, project_three(): jnp.dot(normed, weights[member], preferred_element_type=jnp.float32)  26.2 us
    dot_general x1, matrix products, per_device(): jnp.dot(hidden, output_weight, preferred_element_type=jnp.float32)  25.4 us
  transfers between devices with their start and end apart: 9, of which 7 were waited for; matrix products, arithmetic and copies ran while one was open for 10% of the time, Pallas kernels for 5%

profile of v1, /device:TPU:0, one launch (start us, length us, event | category | flops | bytes accessed | tf_op | source)
XLA Modules:
  0.0 609.9 jit_solution(5145815184745982254)
XLA Ops:
  6.5 2.5 copy.24
  9.0 0.0 all-gather.8.cloned.1.call-start
  9.1 0.7 constant_dynamic-slice_fusion.2
  9.8 1.3 fusion.78
  11.2 81.5 %all-gather.6.cloned.1.call-done = bf16[1024,2048]{1,0:T(8,128)(2,1)} async-done(((bf16[1024,512]{1,0:T(8,128)(2,1)}), bf16[1024,2048]{1,0:T(8,128)(2,1)}) %all-gather.6.cloned.1.call-update) | async-done | bytes 4194320 | tf_op jit(solution)/shard_map/all_gather | solution.py:145
  92.6 3.0 convert_reduce_fusion
  95.6 0.5 copy-done.2
  96.1 1.2 fusion.2
  97.3 1.9 fusion.5
  99.2 3.3 fusion.56.query_ref
  102.5 3.4 fusion.59.key_ref
  106.0 3.3 fusion.62.value_ref
  109.3 18.6 %spatial_attention.1 = bf16[1024,512]{1,0:T(8,128)(2,1)} custom-call(bf16[1024,512]{1,0:T(8,128)(2,1)} %fusion.56.query_ref, bf16[1024,512]{1,0:T(8,128)(2,1)} %fusion.59.key_ref, bf16[1024,512]{1,0:T(8,128)(2,1)} %fusion.62.value_ref), custom_call_target="tpu_custom_call" | custom-call | tf_op jit(solution)/shard_map/spatial_attention/pallas_call | solution.py:44
  127.9 2.3 copy.25
  130.1 3.5 all-to-all-start
  133.7 0.2 all-gather.10.cloned.1.call-start
  133.9 50.9 %all-gather.8.cloned.1.call-done = bf16[2048,2048]{1,0:T(8,128)(2,1)} async-done(((bf16[64,2048]{1,0:T(8,128)(2,1)}), bf16[2048,2048]{1,0:T(8,128)(2,1)}) %all-gather.8.cloned.1.call-update) | async-done | bytes 8388624 | tf_op jit(solution)/shard_map/all_gather | solution.py:111
  184.8 8.3 %copy.26 = bf16[4,8,64,2048]{3,2,1,0:T(8,128)(2,1)} copy(bf16[4,8,64,2048]{3,2,0,1:T(8,128)(2,1)} %bitcast.105) | data formatting | bytes 16777216 | tf_op jit(solution)/shard_map/transpose | solution.py:113
  193.1 6.0 fusion.26
  199.0 18.3 %all_to_all.20 = bf16[8,32,2048]{2,1,0:T(8,128)(2,1)S(1)} all-to-all(bf16[8,32,2048]{2,1,0:T(8,128)(2,1)S(1)} %bitcast.109), channel_id=1, replica_groups=mesh['seq'=8,'head'=4] {'seq'}, dimensions={0} | all-to-all | bytes 2097152 | tf_op jit(solution)/shard_map/all_to_all | solution.py:153
  217.4 0.2 convert_reduce_fusion.2
  217.6 0.1 div.23
  217.7 0.4 multiply_reduce_fusion
  218.1 0.1 rsqrt.29
  218.2 1.4 fusion.43
  219.6 0.0 all-gather.12.cloned.1.call-start
  219.7 1.7 constant_dynamic-slice_fusion.1
  221.4 76.2 %all-gather.10.cloned.1.call-done = bf16[1024,2048]{1,0:T(8,128)(2,1)} async-done(((bf16[256,2048]{1,0:T(8,128)(2,1)}), bf16[1024,2048]{1,0:T(8,128)(2,1)}) %all-gather.10.cloned.1.call-update) | async-done | bytes 4194320 | tf_op jit(solution)/shard_map/all_gather | solution.py:156
  297.6 6.3 %fusion.65 = bf16[1024,512]{1,0:T(8,128)(2,1)} fusion(bf16[1024,2048]{1,0:T(8,128)(2,1)} %all-gather.10.cloned.1.call-done, bf16[3,2048,512]{2,1,0:T(8,128)(2,1)} %param.12), kind=kOutput, calls=%fused_computation.67 | convolution fusion | flops 2148007936 | bytes 7340032 | tf_op jit(solution)/shard_map/dot_general | solution.py:102
  303.9 5.0 fusion.68
  308.9 4.9 fusion.71
  313.8 11.7 %temporal_attention.1 = bf16[4,8,32,512]{3,2,1,0:T(8,128)(2,1)} custom-call(bf16[4,8,32,512]{3,2,1,0:T(8,128)(2,1)} %bitcast.116, bf16[4,8,32,512]{3,2,1,0:T(8,128)(2,1)} %bitcast.117, bf16[4,8,32,512]{3,2,1,0:T(8,128)(2,1)} %bitcast.118), custom_call_target="tpu_custom_call" | custom-call | tf_op jit(solution)/shard_map/temporal_attention/pallas_call | solution.py:90
  325.5 2.3 copy.27
  327.8 3.5 all-to-all-start.2
  331.3 0.3 all-gather.14.cloned.1.call-start
  331.6 56.0 %all-gather.12.cloned.1.call-done = bf16[2048,2048]{1,0:T(8,128)(2,1)} async-done(((bf16[64,2048]{1,0:T(8,128)(2,1)}), bf16[2048,2048]{1,0:T(8,128)(2,1)}) %all-gather.12.cloned.1.call-update) | async-done | bytes 8388624 | tf_op jit(solution)/shard_map/all_gather | solution.py:111
  387.5 8.3 %copy.28 = bf16[4,8,64,2048]{3,2,1,0:T(8,128)(2,1)} copy(bf16[4,8,64,2048]{3,2,0,1:T(8,128)(2,1)} %bitcast.106) | data formatting | bytes 16777216 | tf_op jit(solution)/shard_map/transpose | solution.py:113
  395.8 5.9 convert_reduce_fusion.1
  401.7 0.4 fusion.29
  402.1 1.4 fusion.32
  403.7 79.1 %all-gather.14.cloned.1.call-done = bf16[1024,2048]{1,0:T(8,128)(2,1)} async-done(((bf16[256,2048]{1,0:T(8,128)(2,1)}), bf16[1024,2048]{1,0:T(8,128)(2,1)}) %all-gather.14.cloned.1.call-update) | async-done | bytes 4194320 | tf_op jit(solution)/shard_map/all_gather | solution.py:167
  482.8 25.4 %fusion.20 = bf16[1024,2048]{1,0:T(8,128)(2,1)} fusion(bf16[2048,2048]{1,0:T(8,128)(2,1)} %param.15, bf16[1024,2048]{1,0:T(8,128)(2,1)} %all-gather.14.cloned.1.call-done, bf16[2048,2048]{1,0:T(8,128)(2,1)} %param.14), kind=kOutput, calls=%fused_computation.22 | convolution fusion | flops 17200840704 | bytes 25165824 | tf_op jit(solution)/shard_map/dot_general | solution.py:172
  508.2 1.1 copy.33
  509.3 3.5 all-to-all-start.3
  512.8 54.3 %all-to-all-done.3 = bf16[4,256,512]{2,1,0:T(8,128)(2,1)S(1)} async-done(((bf16[4,256,512]{2,1,0:T(8,128)(2,1)}), bf16[4,256,512]{2,1,0:T(8,128)(2,1)S(1)}, u32[]{:S(2)}, u32[]{:S(2)}) %all-to-all-start.3) | async-done | bytes 1048608 | tf_op jit(solution)/shard_map/all_to_all | solution.py:169
  567.1 33.4 %reduce-scatter.2.cloned.1.call-done = bf16[1024,512]{1,0:T(8,128)(2,1)} async-done(((bf16[1024,2048]{1,0:T(8,128)(2,1)}), bf16[1024,512]{1,0:T(8,128)(2,1)}) %reduce-scatter.2.cloned.1.call-update) | async-done | bytes 1048592 | tf_op jit(solution)/shard_map/reduce_scatter | solution.py:173
  600.5 1.5 fusion.33
  602.0 1.0 copy.30
  (29 shorter events, 0.2 us)
Async XLA Ops:
  6.5 2.5 copy-start
  6.5 86.1 %all-gather.6.cloned.1.call-start = ((), (), s32[]{:S(2)}) async-start(), calls=%async_computation.5 | async-start | bytes 5242880 | tf_op jit(solution)/shard_map/all_gather | solution.py:145
  9.0 175.8 %all-gather.8.cloned.1.call-start = ((), (), s32[]{:S(2)}) async-start(), calls=%async_computation.6 | async-start | bytes 8650752 | tf_op jit(solution)/shard_map/all_gather | solution.py:111
  92.6 3.4 copy-start.2
  96.1 3.1 slice-start
  97.3 1.9 slice-start.1
  130.1 62.9 %all-to-all-start = ((bf16[4,256,512]{1,2,0:T(8,128)(2,1)}), bf16[4,256,512]{1,2,0:T(8,128)(2,1)S(1)}, u32[]{:S(2)}, u32[]{:S(2)}) async-start(bf16[4,256,512]{1,2,0:T(8,128)(2,1)} %copy.25), calls=%async_computation | async-start | bytes 2097152 | tf_op jit(solution)/shard_map/all_to_all | solution.py:119
  133.7 163.9 %all-gather.10.cloned.1.call-start = ((), (), s32[]{:S(2)}) async-start(), calls=%async_computation.7 | async-start | bytes 5242880 | tf_op jit(solution)/shard_map/all_gather | solution.py:156
  219.6 167.9 %all-gather.12.cloned.1.call-start = ((), (), s32[]{:S(2)}) async-start(), calls=%async_computation.8 | async-start | bytes 8650752 | tf_op jit(solution)/shard_map/all_gather | solution.py:111
  297.6 6.3 %copy-start.3 = (bf16[1024,2048]{1,0:T(8,128)(2,1)S(1)}, bf16[1024,2048]{1,0:T(8,128)(2,1)}, u32[]{:S(2)}) copy-start(bf16[1024,2048]{1,0:T(8,128)(2,1)} %all-gather.10.cloned.1.call-done) | copy-start | bytes 12582916
  327.8 68.0 %all-to-all-start.2 = ((bf16[4,256,512]{1,2,0:T(8,128)(2,1)}), bf16[4,256,512]{1,2,0:T(8,128)(2,1)S(1)}, u32[]{:S(2)}, u32[]{:S(2)}) async-start(bf16[4,256,512]{1,2,0:T(8,128)(2,1)} %copy.27), calls=%async_computation.2 | async-start | bytes 2097152 | tf_op jit(solution)/shard_map/all_to_all | solution.py:119
  331.3 151.5 %all-gather.14.cloned.1.call-start = ((), (), s32[]{:S(2)}) async-start(), calls=%async_computation.9 | async-start | bytes 5242880 | tf_op jit(solution)/shard_map/all_gather | solution.py:167
  403.6 196.9 %reduce-scatter.2.cloned.1.call-start = ((), (), s32[]{:S(2)}) async-start(), calls=%async_computation.10 | async-start | bytes 5242880 | tf_op jit(solution)/shard_map/reduce_scatter | solution.py:173
  508.2 94.9 %copy-start.1 = (bf16[512,2048]{1,0:T(8,128)(2,1)S(1)}, bf16[512,2048]{1,0:T(8,128)(2,1)}, u32[]{:S(2)}) copy-start(bf16[512,2048]{1,0:T(8,128)(2,1)} %param.11) | copy-start | bytes 6291460
  509.3 57.8 %all-to-all-start.3 = ((bf16[4,256,512]{2,1,0:T(8,128)(2,1)}), bf16[4,256,512]{2,1,0:T(8,128)(2,1)S(1)}, u32[]{:S(2)}, u32[]{:S(2)}) async-start(bf16[4,256,512]{2,1,0:T(8,128)(2,1)} %bitcast.111), calls=%async_computation.3 | async-start | bytes 2097152 | tf_op jit(solution)/shard_map/all_to_all | solution.py:169
Sparse Core Ops, SparseCore 0:
  9.1 83.4 all-gather.5
  95.6 89.1 all-gather.7
  219.7 77.8 all-gather.9
  300.4 87.0 all-gather.11
  403.7 78.9 all-gather.13
  508.3 92.1 reduce-scatter.1
